TPU v7x, 256 devices: a 8x8x2 block of a 8x8x16 slice. The times are simulated.
256 devices in a mesh: rep: 2 (over z), blk: 128 (over x, y, core).
Axes of the slice: x: 8, y: 8, z: 2, core: 2. Of those that a mesh axis runs over, the one named last changes fastest.
The devices are a block of a 8x8x16 slice.
Arguments:
- hidden: bfloat16 [32, 4096], P('rep', 'blk'), parts along dimension 0, may hold values from -4 to 4
- queries: bfloat16 [32, 4096], P('rep'), parts along dimension 0, may hold values from -180 to 180
- cache_kv: bfloat16 [2, 32, 4096, 1024], P(None, 'rep', 'blk'), parts along dimension 1, may hold values from -6 to 6
- cache_len: int32 [32], P('rep'), parts along dimension 0, may hold values from 1 to 4096
- inserted_key_value: bfloat16 [2, 16, 4096, 1024], P(None, 'rep', 'blk'), parts along dimension 1, may hold values from -6 to 6
- insert_slot: int32 [16], P('rep'), parts along dimension 0, may hold values from 0 to 15, as said below
- prefix_len: int32 [16], P('rep'), parts along dimension 0, may hold values from 1 to 4096, as said below
- out_weight: bfloat16 [4096, 4096], P(None, 'blk'), may hold values from -0.09375 to 0.09375
- norm_gain: bfloat16 [4096], replicated, may hold values from 0.25 to 1.75
- router_weight: bfloat16 [4096, 4], replicated, may hold values from -0.09375 to 0.09375
- expert_ids: int32 [32, 2], P('rep'), parts along dimension 0, may hold values from 0 to 3, all different within a row
- gate_up: bfloat16 [2, 4096, 28672], P(None, None, 'blk'), may hold values from -0.09375 to 0.09375
- down_proj: bfloat16 [28672, 4096], P('blk'), may hold values from -0.0625 to 0.0625
Outputs:
- layer_out: bfloat16 [32, 4096], P('rep', 'blk'), parts along dimension 0
There are 2 independent parts, one for each index of `rep`. A program takes and returns all parts, laid end to end along the dimension named above; an argument that names none is the same for every part. Nothing has to cross between parts.
Inputs may be any that keep to these rules, and one draw needn't show every extreme that they name: `insert_slot`: 8 different slot numbers. `prefix_len`: some inserted request has all 4096 positions.
All inputs are finite; a program needn't handle non-finite values.
Results may differ from a plain program's by a relative error of at most 0.012.
Values may be sent and summed in bfloat16 or wider, within the bound.
A program may use at most 128 MiB of HBM per device.

v0:
```python
import math
import jax
import jax.numpy as jnp
from jax import lax
from jax.sharding import Mesh
from jax.sharding import PartitionSpec as P

QUERY_HEADS = 32
KEY_VALUE_HEADS = 8
HEAD_SIZE = 128
EXPERTS = 4
FF = 7168
BLK = ("blk_0", "blk_1", "blk_2")


def shifted(shard, axis, by):
    count = lax.axis_size(axis)
    return lax.ppermute(shard, axis, [(i, (i + by) % count) for i in range(count)])


def all_in_one(shard, axis):
    leaves = jax.tree.leaves(shard)
    order = sorted(range(len(leaves)), key=lambda k: -leaves[k].size)
    width = (1, *leaves[order[0]].shape)[-1]
    lines = [
        jnp.pad(leaves[k].reshape(-1), (0, -leaves[k].size % width)).reshape(-1, width)
        for k in order
    ]
    both, at, found = (lax.all_gather(jnp.concatenate(lines), axis), 0, {})
    for k, line in zip(order, lines):
        piece = both[:, at : at + len(line)].reshape(len(both), -1)
        found[k] = piece[:, : leaves[k].size].reshape(-1, *leaves[k].shape)
        at += len(line)
    numbers = iter(range(len(leaves)))
    return jax.tree.map(lambda _: found[next(numbers)], shard)


def combined_by_axis(shard, axes, combine):
    for axis in axes:
        pieces = all_in_one(shard, axis)
        shard = jax.tree.map(lambda part: part[0], pieces)
        for k in range(1, lax.axis_size(axis)):
            shard = combine(shard, jax.tree.map(lambda part: part[k], pieces))
    return shard


def sum_in_order(tiles, axes, order):
    inside = tiles.shape[1:]
    tiles = tiles.reshape(*(lax.axis_size(a) for a in axes), *inside)
    tiles = jnp.moveaxis(tiles, order, range(len(axes))).reshape(-1, *inside)
    for k in order:
        tiles = lax.psum_scatter(tiles, axes[k], scatter_dimension=0, tiled=True)
    return tiles[0]


def split_up(shard, dim, count):
    before, after = (shard.shape[:dim], shard.shape[dim + 1 :])
    return jnp.moveaxis(shard.reshape(*before, count, -1, *after), dim, 0)


def summed_rows(shard, axes, order, dim):
    count = lax.axis_size(axes)
    return sum_in_order(split_up(shard, dim, count), axes, order)


def block_attention(queries, key_rows, value_rows, valid):
    slot_list = queries.shape[0]
    query_groups = QUERY_HEADS // KEY_VALUE_HEADS
    heads_of_queries = queries.astype(jnp.float32).reshape(
        slot_list, KEY_VALUE_HEADS, query_groups, HEAD_SIZE
    )
    heads_of_keys = key_rows.astype(jnp.float32).reshape(slot_list, -1, KEY_VALUE_HEADS, HEAD_SIZE)
    heads_of_values = value_rows.astype(jnp.float32).reshape(
        slot_list, -1, KEY_VALUE_HEADS, HEAD_SIZE
    )
    scores = jnp.einsum("skgd,sckd->skgc", heads_of_queries, heads_of_keys) / math.sqrt(HEAD_SIZE)
    masked = valid[:, None, None, :]
    peak = jnp.max(jnp.where(masked, scores, -1e30), axis=-1)
    weights = jnp.where(masked, jnp.exp(scores - peak[..., None]), 0.0)
    totals = jnp.sum(weights, axis=-1)
    partial_value = jnp.einsum("skgc,sckd->skgd", weights, heads_of_values)
    return (
        partial_value.reshape(slot_list, QUERY_HEADS, HEAD_SIZE),
        peak.reshape(slot_list, QUERY_HEADS),
        totals.reshape(slot_list, QUERY_HEADS),
    )


def merge_pair(earlier, later):
    early_out, early_peak, early_total = earlier
    late_out, late_peak, late_total = later
    highest = jnp.maximum(early_peak, late_peak)
    early_scale = jnp.exp(early_peak - highest)
    late_scale = jnp.exp(late_peak - highest)
    merged_out = early_out * early_scale[..., None] + late_out * late_scale[..., None]
    return (merged_out, highest, early_total * early_scale + late_total * late_scale)


def route_shares(normed, router_weight, expert_ids):
    logits = jnp.dot(normed, router_weight, preferred_element_type=jnp.float32)
    chosen = (expert_ids[:, :, None] == jnp.arange(EXPERTS, dtype=jnp.int32)[None, None, :]).astype(
        jnp.float32
    )
    picked = jnp.sum(chosen * logits[:, None, :], axis=-1)
    gates = jax.nn.sigmoid(picked - picked[:, ::-1])
    return jnp.sum(gates[:, :, None] * chosen, axis=1)


def on_device(
    hidden,
    queries,
    cache_kv,
    cache_len,
    inserted_key_value,
    insert_slot,
    prefix_len,
    out_weight,
    norm_gain,
    router_weight,
    expert_ids,
    gate_up,
    down_proj,
):
    cycle_size = lax.axis_size(BLK)
    dev_index = lax.axis_index(BLK)
    half_cycle = cycle_size // 2
    ctx_rows = cache_kv.shape[2]
    arrived = shifted(inserted_key_value, BLK, half_cycle)
    cache = cache_kv.at[:, insert_slot].set(arrived)
    slot_lengths = cache_len.at[insert_slot].set(prefix_len)
    positions = dev_index * ctx_rows + jnp.arange(ctx_rows, dtype=jnp.int32)
    valid = positions[None, :] < slot_lengths[:, None]
    partial_value, peak, totals = block_attention(queries, cache[0], cache[1], valid)
    slot_list = queries.shape[0]
    summed, highest, all_totals = combined_by_axis((partial_value, peak, totals), BLK, merge_pair)
    attn = (
        (summed / all_totals[..., None])
        .reshape(slot_list, QUERY_HEADS * HEAD_SIZE)
        .astype(jnp.bfloat16)
    )
    local_mixed = (
        hidden.astype(jnp.float32) + jnp.dot(attn, out_weight, preferred_element_type=jnp.float32)
    ).astype(jnp.bfloat16)
    mixed = lax.all_gather(local_mixed, BLK, axis=1, tiled=True)
    mixed_f = mixed.astype(jnp.float32)
    scale = lax.rsqrt(jnp.mean(mixed_f * mixed_f, axis=-1, keepdims=True) + 1e-05)
    normed = (mixed_f * scale * norm_gain.astype(jnp.float32)).astype(jnp.bfloat16)
    shares = route_shares(normed, router_weight, expert_ids)
    unit_count = gate_up.shape[2]
    expert_now = dev_index * unit_count // FF
    picker = (jnp.arange(EXPERTS, dtype=jnp.int32) == expert_now).astype(jnp.float32)
    expert_share = jnp.sum(shares * picker[None, :], axis=1)
    act = (
        jax.nn.silu(jnp.dot(normed, gate_up[0], preferred_element_type=jnp.float32))
        * jnp.dot(normed, gate_up[1], preferred_element_type=jnp.float32)
    ).astype(jnp.bfloat16)
    term = expert_share[:, None] * jnp.dot(act, down_proj, preferred_element_type=jnp.float32)
    moe = summed_rows(term, BLK, (2, 0, 1), 1)
    return (local_mixed.astype(jnp.float32) + moe).astype(jnp.bfloat16)


def solution(mesh):
    split = Mesh(
        mesh.devices.reshape(mesh.shape["rep"], 8, 8, 2), ("rep", "blk_0", "blk_1", "blk_2")
    )
    return jax.shard_map(
        on_device,
        mesh=split,
        in_specs=(
            P("rep", BLK),
            P("rep", None),
            P(None, "rep", BLK, None),
            P("rep"),
            P(None, "rep", BLK, None),
            P("rep"),
            P("rep"),
            P(None, BLK),
            P(),
            P(),
            P("rep", None),
            P(None, None, BLK),
            P(BLK, None),
        ),
        out_specs=P("rep", BLK),
        check_vma=False,
    )
```

profile of v0, /device:TPU:514, one launch (start us, length us, event | category | flops | bytes accessed | tf_op | source)
XLA Modules:
  0.0 353.1 jit_solution(5497632940912069190)
XLA Ops:
  6.6 3.3 copy.67
  9.9 5.1 %collective-permute-start = (bf16[2,8,32,1024]{3,2,1,0:T(8,128)(2,1)}, bf16[2,8,32,1024]{3,2,1,0:T(8,128)(2,1)S(1)}, u32[]{:S(2)}, u32[]{:S(2)}) collective-permute-start(bf16[2,8,32,1024]{3,2,1,0:T(8,128)(2,1)} %param.17), channel_id=1, source_target_pairs={{0,64},{1,65},{2,66},{3,67},{4,68},{5,69},{6,70},{7,71},{8,72},{9,... | collective-permute-start | bytes 3145736 | tf_op jit(solution)/shard_map/ppermute | solution.py:18
  15.2 0.6 scatter_fusion
  15.9 44.1 %collective-permute-done = bf16[2,8,32,1024]{3,2,1,0:T(8,128)(2,1)S(1)} collective-permute-done((bf16[2,8,32,1024]{3,2,1,0:T(8,128)(2,1)}, bf16[2,8,32,1024]{3,2,1,0:T(8,128)(2,1)S(1)}, u32[]{:S(2)}, u32[]{:S(2)}) %collective-permute-start) | collective-permute-done | bytes 1048608 | tf_op jit(solution)/shard_map/ppermute | solution.py:18
  60.0 1.0 copy-done.2
  60.9 1.3 copy.39
  62.3 2.9 scatter_fusion.1
  65.1 1.7 fusion.176
  66.9 0.3 copy.46
  67.1 0.3 copy.47
  67.4 0.7 select_reduce_fusion
  68.3 0.4 fusion.62
  68.7 0.4 fusion.15
  69.2 0.7 pad_maximum_fusion
  70.1 61.1 %all-gather.7.cloned.1.call-done = f32[4160,128]{1,0:T(8,128)} async-done(((f32[520,128]{1,0:T(8,128)}), f32[4160,128]{1,0:T(8,128)}) %all-gather.7.cloned.1.call-update) | async-done | bytes 2129936 | tf_op jit(solution)/shard_map/all_gather | solution.py:29
  131.2 0.7 fusion.151
  131.9 0.8 fusion.102
  132.7 0.7 fusion.150
  133.4 0.7 fusion.148
  134.1 0.7 fusion.146
  134.8 2.5 fusion.42
  137.3 0.7 pad_maximum_fusion.1
  138.2 41.5 %all-gather.9.cloned.1.call-done = f32[4160,128]{1,0:T(8,128)} async-done(((f32[520,128]{1,0:T(8,128)}), f32[4160,128]{1,0:T(8,128)}) %all-gather.9.cloned.1.call-update) | async-done | bytes 2129936 | tf_op jit(solution)/shard_map/all_gather | solution.py:29
  179.7 0.7 fusion.136
  180.4 0.8 fusion.81
  181.2 0.7 fusion.135
  181.9 0.7 fusion.133
  182.6 0.7 fusion.131
  183.3 2.5 fusion.21
  185.9 2.4 all-gather.2
  188.9 0.1 mul.560
  189.0 0.1 div.33
  189.1 0.6 fusion.14
  189.8 50.2 %all-gather.3 = bf16[128,32,16]{1,2,0:T(8,128)(2,1)S(1)} all-gather(bf16[1,32,16]{1,2,0:T(8,128)(2,1)S(1)} %bitcast.762), channel_id=1, replica_groups=mesh['rep'=2,'blk_0'=8,'blk_1'=8,'blk_2'=2] {'blk_0','blk_1','blk_2'}, dimensions={0}, use_global_device_ids=true | all-gather | bytes 132096 | tf_op jit(solution)/shard_map/all_gather | solution.py:144
  239.9 0.5 copy.42
  240.5 0.2 copy.43
  240.7 0.5 reshape.962
  241.2 0.1 multiply_reduce_fusion
  241.5 2.1 fusion.2
  243.6 0.2 fusion.179
  243.9 2.9 convolution_multiply_fusion
  246.8 0.3 reshape.936
  247.2 0.6 copy.44
  247.8 1.1 copy.45
  249.0 14.1 %reduce-scatter.4.cloned.1.call-done = f32[64,16,32]{2,1,0:T(8,128)} async-done(((f32[128,16,32]{2,1,0:T(8,128)}), f32[64,16,32]{2,1,0:T(8,128)}) %reduce-scatter.4.cloned.1.call-update) | async-done | bytes 131088 | tf_op jit(solution)/shard_map/reduce_scatter | solution.py:52
  263.3 41.8 %reduce-scatter.6.cloned.1.call-done = f32[8,16,32]{2,1,0:T(8,128)} async-done(((f32[64,16,32]{2,1,0:T(8,128)}), f32[8,16,32]{2,1,0:T(8,128)}) %reduce-scatter.6.cloned.1.call-update) | async-done | bytes 16400 | tf_op jit(solution)/shard_map/reduce_scatter | solution.py:52
  305.1 40.1 %reduce-scatter.8.cloned.1.call-done = f32[1,16,32]{2,1,0:T(8,128)} async-done(((f32[8,16,32]{2,1,0:T(8,128)}), f32[1,16,32]{2,1,0:T(8,128)}) %reduce-scatter.8.cloned.1.call-update) | async-done | bytes 2064 | tf_op jit(solution)/shard_map/reduce_scatter | solution.py:52
  345.3 1.3 fusion.74
  (57 shorter events, 1.9 us)
Async XLA Ops:
  6.5 237.4 %copy-start = (bf16[224,4096]{1,0:T(8,128)(2,1)S(1)}, bf16[224,4096]{1,0:T(8,128)(2,1)}, u32[]{:S(2)}) copy-start(bf16[224,4096]{1,0:T(8,128)(2,1)} %param.25) | copy-start | bytes 5505028
  6.6 8.5 %copy-start.4 = (bf16[16,4096]{1,0:T(8,128)(2,1)S(1)}, bf16[16,4096]{1,0:T(8,128)(2,1)}, u32[]{:S(2)}) copy-start(bf16[16,4096]{1,0:T(8,128)(2,1)} %param.14) | copy-start | bytes 393220
  6.6 124.6 %all-gather.7.cloned.1.call-start = ((), (), s32[]{:S(2)}) async-start(), calls=%async_computation.6 | async-start | bytes 2396160 | tf_op jit(solution)/shard_map/all_gather | solution.py:29
  6.6 8.6 %copy-start.10 = (s32[8]{0:T(128)S(1)}, s32[8]{0:T(128)}, u32[]{:S(2)}) copy-start(s32[8]{0:T(128)} %param.18) | copy-start | bytes 100
  6.6 8.6 %copy-start.1 = (s32[16]{0:T(128)S(1)}, s32[16]{0:T(128)}, u32[]{:S(2)}) copy-start(s32[16]{0:T(128)} %param.16) | copy-start | bytes 196
  6.6 8.6 %copy-start.8 = (s32[8]{0:T(128)S(1)}, s32[8]{0:T(128)}, u32[]{:S(2)}) copy-start(s32[8]{0:T(128)} %param.19) | copy-start | bytes 100
  9.9 50.0 %collective-permute-start = (bf16[2,8,32,1024]{3,2,1,0:T(8,128)(2,1)}, bf16[2,8,32,1024]{3,2,1,0:T(8,128)(2,1)S(1)}, u32[]{:S(2)}, u32[]{:S(2)}) collective-permute-start(bf16[2,8,32,1024]{3,2,1,0:T(8,128)(2,1)} %param.17), channel_id=1, source_target_pairs={{0,64},{1,65},{2,66},{3,67},{4,68},{5,69},{6,70},{7,71},{8,72},{9,... | collective-permute-start | bytes 3145736 | tf_op jit(solution)/shard_map/ppermute | solution.py:18
  59.9 1.0 copy-start.2
  69.1 69.0 %copy-start.5 = (bf16[4096]{0:T(1024)(128)(2,1)S(1)}, bf16[4096]{0:T(1024)(128)(2,1)}, u32[]{:S(2)}) copy-start(bf16[4096]{0:T(1024)(128)(2,1)} %param.21) | copy-start | bytes 24580
  70.0 109.7 %all-gather.9.cloned.1.call-start = ((), (), s32[]{:S(2)}) async-start(), calls=%async_computation.7 | async-start | bytes 2396160 | tf_op jit(solution)/shard_map/all_gather | solution.py:29
  138.1 125.1 %reduce-scatter.4.cloned.1.call-start = ((), (), s32[]{:S(2)}) async-start(), calls=%async_computation.3 | async-start | bytes 1572864 | tf_op jit(solution)/shard_map/reduce_scatter | solution.py:52
  185.8 3.3 copy-start.3
  185.8 3.3 copy-start.6
  240.7 2.9 copy-start.9
  240.7 3.0 copy-start.7
  248.9 56.1 %reduce-scatter.6.cloned.1.call-start = ((), (), s32[]{:S(2)}) async-start(), calls=%async_computation.4 | async-start | bytes 589824 | tf_op jit(solution)/shard_map/reduce_scatter | solution.py:52
  263.2 82.1 %reduce-scatter.8.cloned.1.call-start = ((), (), s32[]{:S(2)}) async-start(), calls=%async_computation.5 | async-start | bytes 73728 | tf_op jit(solution)/shard_map/reduce_scatter | solution.py:52
Sparse Core Ops, SparseCore 0:
  70.1 61.0 all-gather.6
  138.2 41.4 all-gather.8
  249.1 14.0 reduce-scatter.3
  265.5 39.5 reduce-scatter.5
  307.4 37.7 reduce-scatter.7
where the time goes:
time: 354 us; the launch traced here: 353 us
  waiting for transfers between devices  243 us (69%)
  blocking collectives  52.5 us (15%)
  local copies, waits for them, and re-layouts  15.9 us (4%)
  other arithmetic  15.8 us (4%)
  between operations  13.6 us (4%)
  matrix products  6.93 us (2%)
  starting transfers between devices  5.39 us (2%)
    all_gather x2, waiting for transfers between devices, all_in_one(): both, at, found = (lax.all_gather(jnp.concatenate(lines), axis), 0, {})  103 us
    reduce_scatter x3, waiting for transfers between devices, sum_in_order(): tiles = lax.psum_scatter(tiles, axes[k], scatter_dimension=0, tiled=True)  96.1 us
    all_gather x1, blocking collectives, on_device(): mixed = lax.all_gather(local_mixed, BLK, axis=1, tiled=True)  50.2 us
    ppermute x1, waiting for transfers between devices, shifted(): lax.ppermute(shard, axis, [(i, (i + by) % count) for i in range(count)])  44.1 us
  transfers between devices with their start and end apart: 6, of which 6 were waited for; matrix products, arithmetic and copies ran while one was open for 0% of the time, Pallas kernels for 0%

commit v1 on v0

--- a/solution.py
+++ b/solution.py
@@ -11,6 +11,11 @@
 EXPERTS = 4
 FF = 7168
 BLK = ("blk_0", "blk_1", "blk_2")
+
+
+def gather_over(x, axis, d):
+    repeated = jnp.stack([x] * lax.axis_size(axis))
+    return jnp.concatenate(lax.all_to_all(repeated, axis, 0, 0), axis=d)
 
 
 def shifted(shard, axis, by):
@@ -141,7 +146,7 @@
     local_mixed = (
         hidden.astype(jnp.float32) + jnp.dot(attn, out_weight, preferred_element_type=jnp.float32)
     ).astype(jnp.bfloat16)
-    mixed = lax.all_gather(local_mixed, BLK, axis=1, tiled=True)
+    mixed = gather_over(local_mixed, BLK, 1)
     mixed_f = mixed.astype(jnp.float32)
     scale = lax.rsqrt(jnp.mean(mixed_f * mixed_f, axis=-1, keepdims=True) + 1e-05)
     normed = (mixed_f * scale * norm_gain.astype(jnp.float32)).astype(jnp.bfloat16)

time: 354 us -> 327 us (0.924)
  blocking collectives: 52.5 us -> 2.37 us
  starting transfers between devices: 5.39 us -> 18.5 us
  waiting for transfers between devices: 243 us -> 249 us
    all_gather x1 -> x0, blocking collectives: 50.2 us -> none  [on_device(): mixed = lax.all_gather(local_mixed, BLK, axis=1, tiled=True)]
    all_to_all x0 -> x1, starting transfers between devices: none -> 13 us  [gather_over(): return jnp.concatenate(lax.all_to_all(repeated, axis, 0, 0), axis=d)]
    all_to_all x0 -> x1, waiting for transfers between devices: none -> 11 us  [gather_over(): return jnp.concatenate(lax.all_to_all(repeated, axis, 0, 0), axis=d)]
    reduce_scatter x3, waiting for transfers between devices: 96.1 us -> 91.3 us  [sum_in_order(): tiles = lax.psum_scatter(tiles, axes[k], scatter_dimension=0, tiled=True)]
  transfers between devices with their start and end apart: 6 -> 7, of which waited for: 6 -> 7; matrix products, arithmetic and copies ran while one was open for 0% -> 0% of each run, Pallas kernels for 0% -> 0%
where the time goes in v1:
time: 327 us; the launch traced here: 326 us
  waiting for transfers between devices  249 us (76%)
  starting transfers between devices  18.5 us (6%)
  local copies, waits for them, and re-layouts  18.3 us (6%)
  other arithmetic  16.2 us (5%)
  between operations  13.6 us (4%)
  matrix products  7.95 us (2%)
    all_gather x2, waiting for transfers between devices, all_in_one(): both, at, found = (lax.all_gather(jnp.concatenate(lines), axis), 0, {})  103 us
    reduce_scatter x3, waiting for transfers between devices, sum_in_order(): tiles = lax.psum_scatter(tiles, axes[k], scatter_dimension=0, tiled=True)  91.3 us
    ppermute x1, waiting for transfers between devices, shifted(): lax.ppermute(shard, axis, [(i, (i + by) % count) for i in range(count)])  44.1 us
    all_to_all x1, starting transfers between devices, gather_over(): return jnp.concatenate(lax.all_to_all(repeated, axis, 0, 0), axis=d)  13 us
    all_to_all x1, waiting for transfers between devices, gather_over(): return jnp.concatenate(lax.all_to_all(repeated, axis, 0, 0), axis=d)  11 us
  transfers between devices with their start and end apart: 7, of which 7 were waited for; matrix products, arithmetic and copies ran while one was open for 0% of the time, Pallas kernels for 0%

profile of v1, /device:TPU:514, one launch (start us, length us, event | category | flops | bytes accessed | tf_op | source)
XLA Modules:
  0.0 326.2 jit_solution(1636406483602804444)
XLA Ops:
  6.6 3.3 %copy.61 = bf16[2,16,32,1024]{3,2,1,0:T(8,128)(2,1)} copy(bf16[2,16,32,1024]{3,2,1,0:T(8,128)(2,1)} %param.15) | data formatting | bytes 4194304
  9.9 5.1 %collective-permute-start = (bf16[2,8,32,1024]{3,2,1,0:T(8,128)(2,1)}, bf16[2,8,32,1024]{3,2,1,0:T(8,128)(2,1)S(1)}, u32[]{:S(2)}, u32[]{:S(2)}) collective-permute-start(bf16[2,8,32,1024]{3,2,1,0:T(8,128)(2,1)} %param.17), channel_id=1, source_target_pairs={{0,64},{1,65},{2,66},{3,67},{4,68},{5,69},{6,70},{7,71},{8,72},{9,... | collective-permute-start | bytes 3145736 | tf_op jit(solution)/shard_map/ppermute | solution.py:23
  15.2 0.6 scatter_fusion
  15.9 44.1 %collective-permute-done = bf16[2,8,32,1024]{3,2,1,0:T(8,128)(2,1)S(1)} collective-permute-done((bf16[2,8,32,1024]{3,2,1,0:T(8,128)(2,1)}, bf16[2,8,32,1024]{3,2,1,0:T(8,128)(2,1)S(1)}, u32[]{:S(2)}, u32[]{:S(2)}) %collective-permute-start) | collective-permute-done | bytes 1048608 | tf_op jit(solution)/shard_map/ppermute | solution.py:23
  59.9 1.0 copy-done.2
  60.9 1.3 copy.33
  62.2 2.9 scatter_fusion.1
  65.1 1.7 fusion.183
  67.1 0.3 copy.41
  67.4 0.7 select_reduce_fusion
  68.3 0.4 fusion.66
  68.7 0.4 fusion.18
  69.2 0.7 pad_maximum_fusion
  70.1 61.1 %all-gather.6.cloned.1.call-done = f32[4160,128]{1,0:T(8,128)} async-done(((f32[520,128]{1,0:T(8,128)}), f32[4160,128]{1,0:T(8,128)}) %all-gather.6.cloned.1.call-update) | async-done | bytes 2129936 | tf_op jit(solution)/shard_map/all_gather | solution.py:34
  131.2 0.7 fusion.158
  131.8 0.8 fusion.109
  132.7 0.7 fusion.157
  133.4 0.7 fusion.155
  134.1 0.7 fusion.153
  134.8 2.5 fusion.46
  137.3 0.7 pad_maximum_fusion.1
  138.1 41.6 %all-gather.8.cloned.1.call-done = f32[4160,128]{1,0:T(8,128)} async-done(((f32[520,128]{1,0:T(8,128)}), f32[4160,128]{1,0:T(8,128)}) %all-gather.8.cloned.1.call-update) | async-done | bytes 2129936 | tf_op jit(solution)/shard_map/all_gather | solution.py:34
  179.7 0.7 fusion.143
  180.4 0.8 fusion.88
  181.2 0.7 fusion.142
  181.9 0.7 fusion.140
  182.6 0.7 fusion.138
  183.3 2.5 fusion.25
  185.9 2.4 all-gather.2
  189.2 0.6 fusion.14
  189.9 1.0 reshape.987
  190.9 13.0 %all-to-all-start = ((bf16[128,2,256]{2,1,0:T(2,128)(2,1)}), bf16[128,2,256]{2,1,0:T(2,128)(2,1)S(1)}, u32[]{:S(2)}, u32[]{:S(2)}) async-start(bf16[128,2,256]{2,1,0:T(2,128)(2,1)} %reshape.987), calls=%async_computation | async-start | bytes 262144 | tf_op jit(solution)/shard_map/all_to_all | solution.py:18
  204.2 11.0 %all-to-all-done = bf16[128,2,256]{2,1,0:T(2,128)(2,1)S(1)} async-done(((bf16[128,2,256]{2,1,0:T(2,128)(2,1)}), bf16[128,2,256]{2,1,0:T(2,128)(2,1)S(1)}, u32[]{:S(2)}, u32[]{:S(2)}) %all-to-all-start) | async-done | bytes 131104 | tf_op jit(solution)/shard_map/all_to_all | solution.py:18
  215.2 0.3 reshape.988
  215.6 0.3 fusion.15
  215.9 0.3 copy.36
  216.2 1.2 reshape.965
  217.4 1.2 fusion.67
  219.1 0.5 convert_element_type.65
  219.7 2.1 fusion.2
  221.8 2.9 convolution_multiply_fusion
  224.7 0.3 reshape.962
  225.0 0.6 copy.38
  225.6 1.1 copy.39
  226.9 9.2 %reduce-scatter.4.cloned.1.call-done = f32[64,16,32]{2,1,0:T(8,128)} async-done(((f32[128,16,32]{2,1,0:T(8,128)}), f32[64,16,32]{2,1,0:T(8,128)}) %reduce-scatter.4.cloned.1.call-update) | async-done | bytes 131088 | tf_op jit(solution)/shard_map/reduce_scatter | solution.py:57
  236.2 41.8 %reduce-scatter.6.cloned.1.call-done = f32[8,16,32]{2,1,0:T(8,128)} async-done(((f32[64,16,32]{2,1,0:T(8,128)}), f32[8,16,32]{2,1,0:T(8,128)}) %reduce-scatter.6.cloned.1.call-update) | async-done | bytes 16400 | tf_op jit(solution)/shard_map/reduce_scatter | solution.py:57
  278.1 40.2 %reduce-scatter.8.cloned.1.call-done = f32[1,16,32]{2,1,0:T(8,128)} async-done(((f32[8,16,32]{2,1,0:T(8,128)}), f32[1,16,32]{2,1,0:T(8,128)}) %reduce-scatter.8.cloned.1.call-update) | async-done | bytes 2064 | tf_op jit(solution)/shard_map/reduce_scatter | solution.py:57
  318.4 1.3 fusion.81
  (64 shorter events, 3.0 us)
Async XLA Ops:
  6.5 215.2 %copy-start = (bf16[224,4096]{1,0:T(8,128)(2,1)S(1)}, bf16[224,4096]{1,0:T(8,128)(2,1)}, u32[]{:S(2)}) copy-start(bf16[224,4096]{1,0:T(8,128)(2,1)} %param.25) | copy-start | bytes 5505028
  6.6 8.5 %copy-start.4 = (bf16[16,4096]{1,0:T(8,128)(2,1)S(1)}, bf16[16,4096]{1,0:T(8,128)(2,1)}, u32[]{:S(2)}) copy-start(bf16[16,4096]{1,0:T(8,128)(2,1)} %param.14) | copy-start | bytes 393220
  6.6 124.6 %all-gather.6.cloned.1.call-start = ((), (), s32[]{:S(2)}) async-start(), calls=%async_computation.7 | async-start | bytes 2396160 | tf_op jit(solution)/shard_map/all_gather | solution.py:34
  6.6 8.6 %copy-start.10 = (s32[8]{0:T(128)S(1)}, s32[8]{0:T(128)}, u32[]{:S(2)}) copy-start(s32[8]{0:T(128)} %param.18) | copy-start | bytes 100
  6.6 8.6 %copy-start.1 = (s32[16]{0:T(128)S(1)}, s32[16]{0:T(128)}, u32[]{:S(2)}) copy-start(s32[16]{0:T(128)} %param.16) | copy-start | bytes 196
  6.6 8.6 %copy-start.9 = (s32[8]{0:T(128)S(1)}, s32[8]{0:T(128)}, u32[]{:S(2)}) copy-start(s32[8]{0:T(128)} %param.19) | copy-start | bytes 100
  9.9 50.0 %collective-permute-start = (bf16[2,8,32,1024]{3,2,1,0:T(8,128)(2,1)}, bf16[2,8,32,1024]{3,2,1,0:T(8,128)(2,1)S(1)}, u32[]{:S(2)}, u32[]{:S(2)}) collective-permute-start(bf16[2,8,32,1024]{3,2,1,0:T(8,128)(2,1)} %param.17), channel_id=1, source_target_pairs={{0,64},{1,65},{2,66},{3,67},{4,68},{5,69},{6,70},{7,71},{8,72},{9,... | collective-permute-start | bytes 3145736 | tf_op jit(solution)/shard_map/ppermute | solution.py:23
  59.9 1.0 copy-start.2
  70.0 109.7 %all-gather.8.cloned.1.call-start = ((), (), s32[]{:S(2)}) async-start(), calls=%async_computation.8 | async-start | bytes 2396160 | tf_op jit(solution)/shard_map/all_gather | solution.py:34
  185.8 3.3 %copy-start.3 = (bf16[4096,32]{0,1:T(8,128)(2,1)S(1)}, bf16[4096,32]{0,1:T(8,128)(2,1)}, u32[]{:S(2)}) copy-start(bf16[4096,32]{0,1:T(8,128)(2,1)} %param.20) | copy-start | bytes 786436
  185.8 3.3 %copy-start.7 = (bf16[16,32]{1,0:T(8,128)(2,1)S(1)}, bf16[16,32]{1,0:T(8,128)(2,1)}, u32[]{:S(2)}) copy-start(bf16[16,32]{1,0:T(8,128)(2,1)} %param.13) | copy-start | bytes 3076
  188.3 15.8 %copy-start.6 = (bf16[4096]{0:T(1024)(128)(2,1)S(1)}, bf16[4096]{0:T(1024)(128)(2,1)}, u32[]{:S(2)}) copy-start(bf16[4096]{0:T(1024)(128)(2,1)} %param.21) | copy-start | bytes 24580
  190.9 24.3 %all-to-all-start = ((bf16[128,2,256]{2,1,0:T(2,128)(2,1)}), bf16[128,2,256]{2,1,0:T(2,128)(2,1)S(1)}, u32[]{:S(2)}, u32[]{:S(2)}) async-start(bf16[128,2,256]{2,1,0:T(2,128)(2,1)} %reshape.987), calls=%async_computation | async-start | bytes 262144 | tf_op jit(solution)/shard_map/all_to_all | solution.py:18
  203.9 32.2 %reduce-scatter.4.cloned.1.call-start = ((), (), s32[]{:S(2)}) async-start(), calls=%async_computation.4 | async-start | bytes 1572864 | tf_op jit(solution)/shard_map/reduce_scatter | solution.py:57
  215.6 1.9 copy-start.5
  215.6 3.0 copy-start.8
  226.8 51.3 %reduce-scatter.6.cloned.1.call-start = ((), (), s32[]{:S(2)}) async-start(), calls=%async_computation.5 | async-start | bytes 589824 | tf_op jit(solution)/shard_map/reduce_scatter | solution.py:57
  236.2 82.2 %reduce-scatter.8.cloned.1.call-start = ((), (), s32[]{:S(2)}) async-start(), calls=%async_computation.6 | async-start | bytes 73728 | tf_op jit(solution)/shard_map/reduce_scatter | solution.py:57
Sparse Core Ops, SparseCore 0:
  70.1 60.9 all-gather.5
  138.2 41.4 all-gather.7
  226.9 9.1 reduce-scatter.3
  238.5 39.5 reduce-scatter.5
  280.4 37.9 reduce-scatter.7
